TPU v7x, 32 devices: a whole 2x2x4 slice. The times are simulated.
32 devices in a mesh: section: 4 (over z), dp: 8 (over y, x, core).
Axes of the slice: x: 2, y: 2, z: 4, core: 2. Of those that a mesh axis runs over, the one named last changes fastest.
Arguments:
- stream: float32 [2, 64, 16, 16, 128], P(None, 'dp'), may hold values from -6 to 6
- cotangent: float32 [2, 64, 16, 16, 128], P(None, 'dp'), may hold values from -6 to 6
- weights: bfloat16 [4, 2304, 128], P('section'), may hold values from -0.09375 to 0.09375
- master: float32 [4, 2304, 128], P('section', 'dp'), may hold values from -0.09375 to 0.09375
- momentum: float32 [4, 2304, 128], P('section', 'dp'), may hold values from -6 to 6
Outputs:
- new_master: float32 [4, 2304, 128], P('section', 'dp')
- new_momentum: float32 [4, 2304, 128], P('section', 'dp')
- new_weights: bfloat16 [4, 2304, 128], P('section')
All inputs are finite; a program needn't handle non-finite values.
Results may differ from a plain program's by a relative error of at most 0.014.
Values may be sent and summed in bfloat16 or wider, within the bound.
A program may use at most 64 MiB of HBM per device.

v0:
```python
import functools
import math

import jax
import jax.numpy as jnp
from jax import lax
from jax.experimental import pallas as pl
from jax.experimental.pallas import tpu as pltpu
from jax.sharding import PartitionSpec as P

MESH = pl.DeviceIdType.MESH
step_size = 0.1
inertia = 0.9


def kernel(
    S, D, images,
    stream, cotangent, weights, master, momentum,
    new_master, new_momentum, new_weights,
    wbuf, xs, ds, pads, kept, slopes, g32, gsend, pairs, recv1, zsend, recv2, gown, spread_out,
    in_sem, own_sem, w1send, w1recv, w2send, w2recv, w3send, w3recv,
    psend, precv, gsend_sem, grecv_sem, zsend_sem, zrecv_sem,
    osend_sem, orecv_sem, fsend_sem, frecv_sem,
):
    s = lax.axis_index("section")
    d = lax.axis_index("dp")
    core = lax.rem(d, 2)
    partner = d + 1 - 2 * core
    chips = D // 2
    share, H, W, C = xs.shape[1:]
    M = share * H * W
    rows = master.shape[0]
    R = rows * D
    NC = math.gcd(R // 16, D)
    part = R // NC

    def chunk(i):
        return pl.ds(pl.multiple_of(i * part, 16), part)

    def other_chip(i):
        return lax.rem(d + 2 * i, D)

    def section_copy(src, to):
        return pltpu.make_async_remote_copy(
            src_ref=weights.at[chunk(d)], dst_ref=wbuf.at[src, chunk(d)],
            send_sem=w1send.at[to], recv_sem=w1recv.at[src],
            device_id=(to, d), device_id_type=MESH)

    def layer_copy(sec, src, to):
        return pltpu.make_async_remote_copy(
            src_ref=wbuf.at[sec, chunk(src)], dst_ref=wbuf.at[sec, chunk(src)],
            send_sem=w2send.at[sec, to], recv_sem=w2recv.at[sec, src],
            device_id=(s, to), device_id_type=MESH)

    def core_copy(sec, src):
        return pltpu.make_async_remote_copy(
            src_ref=wbuf.at[sec, chunk(src)], dst_ref=wbuf.at[sec, chunk(src)],
            send_sem=w3send.at[sec, src], recv_sem=w3recv.at[sec, src],
            device_id=(s, partner), device_id_type=MESH)

    @pl.when(d < NC)
    def _():
        for i in range(1, S):
            section_copy(s, lax.rem(s + i, S)).start()

    load_own = pltpu.make_async_copy(weights, wbuf.at[s], own_sem)
    load_own.start()
    mine = pl.ds(s * share, share)
    loads = [
        pltpu.make_async_copy(stream.at[0, mine], xs.at[0], in_sem.at[0]),
        pltpu.make_async_copy(stream.at[1, mine], xs.at[1], in_sem.at[1]),
        pltpu.make_async_copy(cotangent.at[0, mine], ds.at[0], in_sem.at[2]),
        pltpu.make_async_copy(cotangent.at[1, mine], ds.at[1], in_sem.at[3]),
    ]
    for load in loads:
        load.start()

    zero_row = jnp.zeros((share, 1, W, 3 * C), jnp.bfloat16)
    for k in range(2):
        pads[k, :, 0:1] = zero_row
        pads[k, :, H + 1 : H + 2] = zero_row

    col = lax.rem(lax.broadcasted_iota(jnp.int32, (M, C), 0), W)

    def shifted(k, flat, order):
        before = jnp.where(col == 0, 0.0, pltpu.roll(flat, 1, 0))
        after = jnp.where(col == W - 1, 0.0, pltpu.roll(flat, M - 1, 0))
        for b, piece in enumerate((before, flat, after) if order else (after, flat, before)):
            pads[k, :, 1 : H + 1, :, b * C : (b + 1) * C] = piece.astype(jnp.bfloat16).reshape(
                share, H, W, C)

    def activate(value, sec, which):
        logistic = 1.0 / (1.0 + jnp.exp(-value))
        act = value * logistic
        slopes[sec, which] = logistic * (1.0 + value * (1.0 - logistic))
        kept[sec, which] = act.astype(jnp.bfloat16)
        shifted(0, act, True)

    def conv(sec, which):
        total = jnp.zeros((M, C), jnp.float32)
        for a in range(3):
            total += jnp.dot(
                pads[0, :, a : a + H].reshape(M, 3 * C),
                wbuf[sec, which * 9 * C + a * 3 * C : which * 9 * C + (a + 1) * 3 * C],
                preferred_element_type=jnp.float32)
        return total

    def relay(sec):
        @pl.when((sec != s) & (d < NC))
        def _():
            section_copy(sec, s).wait_recv()
            layer_copy(sec, d, partner).start()

            @pl.loop(1, chips)
            def _(i):
                layer_copy(sec, d, other_chip(i)).start()

    def pass_on(sec):
        @pl.when(sec != s)
        def _():
            @pl.loop(1, chips)
            def _(i):
                src = other_chip(i)

                @pl.when(src < NC)
                def _():
                    layer_copy(sec, src, d).wait_recv()
                    core_copy(sec, src).start()

    def take(sec):
        @pl.when(sec != s)
        def _():
            @pl.when(partner < NC)
            def _():
                layer_copy(sec, partner, d).wait_recv()

            @pl.loop(1, chips)
            def _(i):
                src = lax.rem(partner + 2 * i, D)

                @pl.when(src < NC)
                def _():
                    core_copy(sec, src).wait_recv()

    load_own.wait()
    for load in loads:
        load.wait()
    for sec in range(S):
        relay(sec)
    pass_on(0)

    def forward_one(sec, carry):
        first = xs[0].reshape(M, C)
        second = xs[1].reshape(M, C)
        activate(second, sec, 0)
        take(sec)
        first = first + conv(sec, 0)
        activate(first, sec, 1)
        xs[0] = first.reshape(share, H, W, C)

        @pl.when(sec + 1 < S)
        def _():
            pass_on(sec + 1)

        xs[1] = (second + conv(sec, 1)).reshape(share, H, W, C)
        return carry

    lax.fori_loop(0, S, forward_one, 0)

    def pair_copy(sec, to):
        return pltpu.make_async_remote_copy(
            src_ref=gsend.at[sec, to], dst_ref=pairs.at[sec, to],
            send_sem=psend.at[sec, to], recv_sem=precv.at[sec, to],
            device_id=(s, partner), device_id_type=MESH)

    def grad_copy(sec, src, to):
        return pltpu.make_async_remote_copy(
            src_ref=gsend.at[sec, to], dst_ref=recv1.at[sec, src],
            send_sem=gsend_sem.at[sec, to], recv_sem=grecv_sem.at[sec, src],
            device_id=(s, to), device_id_type=MESH)

    def sum_copy(sec, src):
        return pltpu.make_async_remote_copy(
            src_ref=zsend.at[sec], dst_ref=recv2.at[src],
            send_sem=zsend_sem.at[sec], recv_sem=zrecv_sem.at[src],
            device_id=(sec, d), device_id_type=MESH)

    def grads(sec, which):
        rounded = ds[1 if which else 0].reshape(M, C)
        shifted(1, rounded, False)
        act = kept[sec, which]
        for a in range(3):
            block = lax.dot_general(
                act, pads[1, :, 2 - a : 2 - a + H].reshape(M, 3 * C),
                (((0,), (0,)), ((), ())), preferred_element_type=jnp.float32)
            for b in range(3):
                g32[(3 * a + b) * C : (3 * a + b + 1) * C] = block[:, b * C : (b + 1) * C]
        per = D // 2

        def convert(at):
            gsend[sec, which * per + at] = g32[
                pl.ds(pl.multiple_of(at * rows, 8), rows)].astype(jnp.bfloat16)

        @pl.loop(0, per // 2)
        def _(i):
            at = 2 * i + 1 - core
            convert(at)
            pair_copy(sec, which * per + at).start()

        @pl.loop(0, per // 2)
        def _(i):
            convert(2 * i + core)

        total = jnp.zeros((M, C), jnp.float32)
        for a in range(3):
            for b in range(3):
                tap = 3 * a + b
                total += lax.dot_general(
                    pads[1, :, 2 - a : 2 - a + H, :, b * C : (b + 1) * C].reshape(M, C),
                    wbuf[sec, which * 9 * C + tap * C : which * 9 * C + (tap + 1) * C],
                    (((1,), (1,)), ((), ())), preferred_element_type=jnp.float32)
        into = 0 if which else 1
        ds[into] = ds[into] + (total * slopes[sec, which]).reshape(share, H, W, C)

    def combine(sec, which):
        per = D // 2

        @pl.loop(0, per // 2)
        def _(i):
            to = which * per + 2 * i + core
            pair_copy(sec, to).wait_recv()
            both = gsend[sec, to].astype(jnp.float32) + pairs[sec, to].astype(jnp.float32)
            gsend[sec, to] = both.astype(jnp.bfloat16)

            @pl.when(to != d)
            def _():
                grad_copy(sec, d, to).start()

    def finish(sec):
        def add(i, total):
            src = other_chip(i)
            grad_copy(sec, src, d).wait_recv()
            return total + recv1[sec, src].astype(jnp.float32)

        total = lax.fori_loop(1, chips, add, gsend[sec, d].astype(jnp.float32))

        @pl.when(sec == s)
        def _():
            gown[...] = total

        @pl.when(sec != s)
        def _():
            zsend[sec] = total.astype(jnp.bfloat16)
            sum_copy(sec, s).start()

    def backward_one(turn, carry):
        sec = S - 1 - turn
        grads(sec, 1)
        combine(sec, 1)

        @pl.when(turn > 0)
        def _():
            finish(sec + 1)

        grads(sec, 0)
        combine(sec, 0)
        return carry

    lax.fori_loop(0, S, backward_one, 0)
    finish(0)

    def gather_sums(i, total):
        src = lax.rem(s + i, S)
        sum_copy(s, src).wait_recv()
        return total + recv2[src].astype(jnp.float32)

    summed = lax.fori_loop(1, S, gather_sums, gown[...])
    moved = inertia * momentum[...] + summed / images
    new_momentum[...] = moved
    fresh = master[...] - step_size * moved
    new_master[...] = fresh
    spread_out[d] = fresh.astype(jnp.bfloat16)

    def out_copy(src, to):
        return pltpu.make_async_remote_copy(
            src_ref=spread_out.at[src], dst_ref=spread_out.at[src],
            send_sem=osend_sem.at[to], recv_sem=orecv_sem.at[src],
            device_id=(s, to), device_id_type=MESH)

    def hand_over(src):
        return pltpu.make_async_remote_copy(
            src_ref=spread_out.at[src], dst_ref=spread_out.at[src],
            send_sem=fsend_sem.at[src], recv_sem=frecv_sem.at[src],
            device_id=(s, partner), device_id_type=MESH)

    @pl.loop(1, chips)
    def _(i):
        out_copy(d, other_chip(i)).start()

    out_copy(d, partner).start()

    @pl.loop(1, S)
    def _(i):
        other = lax.rem(s + i, S)
        sum_copy(other, s).wait_send()

        @pl.when(d < NC)
        def _():
            section_copy(s, other).wait_send()
            layer_copy(other, d, partner).wait_send()

        @pl.loop(1, chips)
        def _(j):
            @pl.when(d < NC)
            def _():
                layer_copy(other, d, other_chip(j)).wait_send()

            @pl.when(other_chip(j) < NC)
            def _():
                core_copy(other, other_chip(j)).wait_send()

    @pl.loop(0, S)
    def _(sec):
        @pl.loop(1, chips)
        def _(i):
            grad_copy(sec, d, other_chip(i)).wait_send()

        @pl.loop(0, chips)
        def _(i):
            pair_copy(sec, 2 * i + 1 - core).wait_send()

    @pl.loop(1, chips)
    def _(i):
        src = other_chip(i)
        out_copy(src, d).wait_recv()
        hand_over(src).start()

    out_copy(partner, d).wait_recv()
    out_copy(d, partner).wait_send()

    @pl.loop(1, chips)
    def _(i):
        out_copy(d, other_chip(i)).wait_send()
        hand_over(other_chip(i)).wait_send()
        hand_over(lax.rem(partner + 2 * i, D)).wait_recv()

    new_weights[...] = spread_out[...]


def on_device(S, D, stream, cotangent, weights, master, momentum):
    _, per_dp, H, W, C = stream.shape
    share = per_dp // S
    M = share * H * W
    R = weights.shape[1]
    rows = master.shape[1]
    bf, f32 = jnp.bfloat16, jnp.float32
    vmem = pl.BlockSpec(memory_space=pltpu.VMEM)
    hbm = pl.BlockSpec(memory_space=pl.ANY)
    dma = pltpu.SemaphoreType.DMA
    new_master, new_momentum, new_weights = pl.pallas_call(
        functools.partial(kernel, S, D, per_dp * D),
        out_shape=(
            jax.ShapeDtypeStruct((rows, C), f32),
            jax.ShapeDtypeStruct((rows, C), f32),
            jax.ShapeDtypeStruct((D, rows, C), bf),
        ),
        in_specs=[hbm, hbm, hbm, vmem, vmem],
        out_specs=(vmem, vmem, vmem),
        scratch_shapes=[
            pltpu.VMEM((S, R, C), bf),
            pltpu.VMEM((2, share, H, W, C), f32),
            pltpu.VMEM((2, share, H, W, C), f32),
            pltpu.VMEM((2, share, H + 2, W, 3 * C), bf),
            pltpu.VMEM((S, 2, M, C), bf),
            pltpu.VMEM((S, 2, M, C), f32),
            pltpu.VMEM((R // 2, C), f32),
            pltpu.VMEM((S, D, rows, C), bf),
            pltpu.VMEM((S, D, rows, C), bf),
            pltpu.VMEM((S, D, rows, C), bf),
            pltpu.VMEM((S, rows, C), bf),
            pltpu.VMEM((S, rows, C), bf),
            pltpu.VMEM((rows, C), f32),
            pltpu.VMEM((D, rows, C), bf),
            dma((4,)), dma, dma((S,)), dma((S,)), dma((S, D)), dma((S, D)), dma((S, D)), dma((S, D)),
            dma((S, D)), dma((S, D)), dma((S, D)), dma((S, D)), dma((S,)), dma((S,)),
            dma((D,)), dma((D,)), dma((D,)), dma((D,)),
        ],
        compiler_params=pltpu.CompilerParams(
            has_side_effects=True, vmem_limit_bytes=61 * 1024 * 1024),
    )(stream, cotangent, weights[0], master[0], momentum[0])
    return (new_master[None], new_momentum[None], new_weights.reshape(1, R, C))


def solution(mesh):
    placed = (
        P(None, "dp", None, None, None),
        P(None, "dp", None, None, None),
        P("section", None, None),
        P("section", "dp", None),
        P("section", "dp", None),
    )
    return jax.shard_map(
        functools.partial(on_device, mesh.shape["section"], mesh.shape["dp"]),
        mesh=mesh,
        in_specs=placed,
        out_specs=(P("section", "dp", None), P("section", "dp", None), P("section", None, None)),
        check_vma=False,
    )
```

profile of v0, /device:TPU:0, one launch (start us, length us, event | category | flops | bytes accessed | tf_op | source)
XLA Modules:
  0.0 76.2 jit_solution(3167606085612372467)
XLA Ops:
  0.6 70.5 %shard_map.76 = (f32[288,128]{1,0:T(8,128)}, f32[288,128]{1,0:T(8,128)}, bf16[8,288,128]{2,1,0:T(8,128)(2,1)}) custom-call(f32[2,8,16,16,128]{4,3,2,1,0:T(8,128)} %stream.1, f32[2,8,16,16,128]{4,3,2,1,0:T(8,128)} %cotangent.1, bf16[2304,128]{1,0:T(8,128)(2,1)} %bitcast.6, f32[288,128]{1,0:T(8,128)} %bitcast.8, f32[288,128]{1,0:T(8,128)} %bitcast.9), custom_call_target="tpu_custom_call" | custom-call | tf_op jit(solution)/shard_map/pallas_call | solution.py:360
  71.1 1.6 %copy.11 = f32[1,288,128]{2,1,0:T(8,128)} copy(f32[1,288,128]{2,1,0:T(8,128)} %bitcast.11) | data formatting | bytes 294912
  72.7 1.6 %copy.12 = f32[1,288,128]{2,1,0:T(8,128)} copy(f32[1,288,128]{2,1,0:T(8,128)} %bitcast.10) | data formatting | bytes 294912
  74.3 1.9 %copy.13 = bf16[1,2304,128]{2,1,0:T(8,128)(2,1)} copy(bf16[1,2304,128]{2,1,0:T(8,128)(2,1)} %bitcast.7) | data formatting | bytes 1179648
where the time goes:
time: 76.4 us; the launch traced here: 76.2 us
  Pallas kernels  70.5 us (92%)
  local copies, waits for them, and re-layouts  5.08 us (7%)
    pallas_call x1, Pallas kernels, on_device(): pl.pallas_call(functools.partial(kernel, S, D, per_dp * D), out_shape=(ja...  70.5 us
    unnamed x3, local copies, waits for them, and re-layouts  5.08 us

commit v1 on v0

--- a/solution.py
+++ b/solution.py
@@ -17,7 +17,7 @@
     S, D, images,
     stream, cotangent, weights, master, momentum,
     new_master, new_momentum, new_weights,
-    wbuf, xs, ds, pads, kept, slopes, g32, gsend, pairs, recv1, zsend, recv2, gown, spread_out,
+    wbuf, xs, ds, pads, kept, slopes, g32, gsend, pairs, recv1, zsend, recv2, gown, spread_out, old_master, old_momentum,
     in_sem, own_sem, w1send, w1recv, w2send, w2recv, w3send, w3recv,
     psend, precv, gsend_sem, grecv_sem, zsend_sem, zrecv_sem,
     osend_sem, orecv_sem, fsend_sem, frecv_sem,
@@ -58,10 +58,15 @@
             send_sem=w3send.at[sec, src], recv_sem=w3recv.at[sec, src],
             device_id=(s, partner), device_id_type=MESH)
 
-    @pl.when(d < NC)
-    def _():
-        for i in range(1, S):
-            section_copy(s, lax.rem(s + i, S)).start()
+    barrier = pltpu.get_barrier_semaphore()
+
+    @pl.loop(1, S)
+    def _(i):
+        pl.semaphore_signal(barrier, inc=1, device_id=(lax.rem(s + i, S), d), device_id_type=MESH)
+
+    @pl.loop(1, D)
+    def _(i):
+        pl.semaphore_signal(barrier, inc=1, device_id=(s, lax.rem(d + i, D)), device_id_type=MESH)
 
     load_own = pltpu.make_async_copy(weights, wbuf.at[s], own_sem)
     load_own.start()
@@ -74,6 +79,19 @@
     ]
     for load in loads:
         load.start()
+    states = [
+        pltpu.make_async_copy(momentum, old_momentum, in_sem.at[4]),
+        pltpu.make_async_copy(master, old_master, in_sem.at[5]),
+    ]
+    for load in states:
+        load.start()
+    with jax.named_scope("t_bar"):
+        pl.semaphore_wait(barrier, S + D - 2)
+
+    @pl.when(d < NC)
+    def _():
+        for i in range(1, S):
+            section_copy(s, lax.rem(s + i, S)).start()
 
     zero_row = jnp.zeros((share, 1, W, 3 * C), jnp.bfloat16)
     for k in range(2):
@@ -142,27 +160,32 @@
                 def _():
                     core_copy(sec, src).wait_recv()
 
-    load_own.wait()
-    for load in loads:
-        load.wait()
-    for sec in range(S):
-        relay(sec)
-    pass_on(0)
+    with jax.named_scope("t_start"):
+        load_own.wait()
+        for load in loads:
+            load.wait()
+        for sec in range(S):
+            relay(sec)
+        pass_on(0)
 
     def forward_one(sec, carry):
         first = xs[0].reshape(M, C)
         second = xs[1].reshape(M, C)
-        activate(second, sec, 0)
-        take(sec)
-        first = first + conv(sec, 0)
-        activate(first, sec, 1)
+        with jax.named_scope("t_act_take"):
+            activate(second, sec, 0)
+            take(sec)
+        with jax.named_scope("t_conv0"):
+            first = first + conv(sec, 0)
+        with jax.named_scope("t_act1"):
+            activate(first, sec, 1)
         xs[0] = first.reshape(share, H, W, C)
 
         @pl.when(sec + 1 < S)
         def _():
             pass_on(sec + 1)
 
-        xs[1] = (second + conv(sec, 1)).reshape(share, H, W, C)
+        with jax.named_scope("t_conv1"):
+            xs[1] = (second + conv(sec, 1)).reshape(share, H, W, C)
         return carry
 
     lax.fori_loop(0, S, forward_one, 0)
@@ -186,41 +209,44 @@
             device_id=(sec, d), device_id_type=MESH)
 
     def grads(sec, which):
-        rounded = ds[1 if which else 0].reshape(M, C)
-        shifted(1, rounded, False)
-        act = kept[sec, which]
-        for a in range(3):
-            block = lax.dot_general(
-                act, pads[1, :, 2 - a : 2 - a + H].reshape(M, 3 * C),
-                (((0,), (0,)), ((), ())), preferred_element_type=jnp.float32)
-            for b in range(3):
-                g32[(3 * a + b) * C : (3 * a + b + 1) * C] = block[:, b * C : (b + 1) * C]
+        with jax.named_scope("t_wgrad"):
+            rounded = ds[1 if which else 0].reshape(M, C)
+            shifted(1, rounded, False)
+            act = kept[sec, which]
+            for a in range(3):
+                block = lax.dot_general(
+                    act, pads[1, :, 2 - a : 2 - a + H].reshape(M, 3 * C),
+                    (((0,), (0,)), ((), ())), preferred_element_type=jnp.float32)
+                for b in range(3):
+                    g32[(3 * a + b) * C : (3 * a + b + 1) * C] = block[:, b * C : (b + 1) * C]
         per = D // 2
 
         def convert(at):
             gsend[sec, which * per + at] = g32[
                 pl.ds(pl.multiple_of(at * rows, 8), rows)].astype(jnp.bfloat16)
 
-        @pl.loop(0, per // 2)
-        def _(i):
-            at = 2 * i + 1 - core
-            convert(at)
-            pair_copy(sec, which * per + at).start()
-
-        @pl.loop(0, per // 2)
-        def _(i):
-            convert(2 * i + core)
-
-        total = jnp.zeros((M, C), jnp.float32)
-        for a in range(3):
-            for b in range(3):
-                tap = 3 * a + b
-                total += lax.dot_general(
-                    pads[1, :, 2 - a : 2 - a + H, :, b * C : (b + 1) * C].reshape(M, C),
-                    wbuf[sec, which * 9 * C + tap * C : which * 9 * C + (tap + 1) * C],
-                    (((1,), (1,)), ((), ())), preferred_element_type=jnp.float32)
-        into = 0 if which else 1
-        ds[into] = ds[into] + (total * slopes[sec, which]).reshape(share, H, W, C)
+        with jax.named_scope("t_convert"):
+            @pl.loop(0, per // 2)
+            def _(i):
+                at = 2 * i + 1 - core
+                convert(at)
+                pair_copy(sec, which * per + at).start()
+
+            @pl.loop(0, per // 2)
+            def _(i):
+                convert(2 * i + core)
+
+        with jax.named_scope("t_dgrad"):
+            total = jnp.zeros((M, C), jnp.float32)
+            for a in range(3):
+                for b in range(3):
+                    tap = 3 * a + b
+                    total += lax.dot_general(
+                        pads[1, :, 2 - a : 2 - a + H, :, b * C : (b + 1) * C].reshape(M, C),
+                        wbuf[sec, which * 9 * C + tap * C : which * 9 * C + (tap + 1) * C],
+                        (((1,), (1,)), ((), ())), preferred_element_type=jnp.float32)
+            into = 0 if which else 1
+            ds[into] = ds[into] + (total * slopes[sec, which]).reshape(share, H, W, C)
 
     def combine(sec, which):
         per = D // 2
@@ -256,30 +282,37 @@
     def backward_one(turn, carry):
         sec = S - 1 - turn
         grads(sec, 1)
-        combine(sec, 1)
-
-        @pl.when(turn > 0)
-        def _():
-            finish(sec + 1)
+        with jax.named_scope("t_comb1"):
+            combine(sec, 1)
+
+        with jax.named_scope("t_fin"):
+            @pl.when(turn > 0)
+            def _():
+                finish(sec + 1)
 
         grads(sec, 0)
-        combine(sec, 0)
+        with jax.named_scope("t_comb0"):
+            combine(sec, 0)
         return carry
 
     lax.fori_loop(0, S, backward_one, 0)
-    finish(0)
+    with jax.named_scope("t_finish0"):
+        finish(0)
 
     def gather_sums(i, total):
         src = lax.rem(s + i, S)
         sum_copy(s, src).wait_recv()
         return total + recv2[src].astype(jnp.float32)
 
-    summed = lax.fori_loop(1, S, gather_sums, gown[...])
-    moved = inertia * momentum[...] + summed / images
-    new_momentum[...] = moved
-    fresh = master[...] - step_size * moved
-    new_master[...] = fresh
-    spread_out[d] = fresh.astype(jnp.bfloat16)
+    with jax.named_scope("t_sum"):
+        summed = lax.fori_loop(1, S, gather_sums, gown[...])
+        for load in states:
+            load.wait()
+        moved = inertia * old_momentum[...] + summed / images
+        new_momentum[...] = moved
+        fresh = old_master[...] - step_size * moved
+        new_master[...] = fresh
+        spread_out[d] = fresh.astype(jnp.bfloat16)
 
     def out_copy(src, to):
         return pltpu.make_async_remote_copy(
@@ -293,58 +326,71 @@
             send_sem=fsend_sem.at[src], recv_sem=frecv_sem.at[src],
             device_id=(s, partner), device_id_type=MESH)
 
-    @pl.loop(1, chips)
-    def _(i):
-        out_copy(d, other_chip(i)).start()
-
-    out_copy(d, partner).start()
-
-    @pl.loop(1, S)
-    def _(i):
-        other = lax.rem(s + i, S)
-        sum_copy(other, s).wait_send()
-
-        @pl.when(d < NC)
-        def _():
-            section_copy(s, other).wait_send()
-            layer_copy(other, d, partner).wait_send()
-
+    with jax.named_scope("t_out"):
         @pl.loop(1, chips)
-        def _(j):
+        def _(i):
+            out_copy(d, other_chip(i)).start()
+
+        out_copy(d, partner).start()
+
+        @pl.loop(1, S)
+        def _(i):
+            other = lax.rem(s + i, S)
+            sum_copy(other, s).wait_send()
+
             @pl.when(d < NC)
             def _():
-                layer_copy(other, d, other_chip(j)).wait_send()
-
-            @pl.when(other_chip(j) < NC)
-            def _():
-                core_copy(other, other_chip(j)).wait_send()
-
-    @pl.loop(0, S)
-    def _(sec):
+                section_copy(s, other).wait_send()
+                layer_copy(other, d, partner).wait_send()
+
+            @pl.loop(1, chips)
+            def _(j):
+                @pl.when(d < NC)
+                def _():
+                    layer_copy(other, d, other_chip(j)).wait_send()
+
+                @pl.when(other_chip(j) < NC)
+                def _():
+                    core_copy(other, other_chip(j)).wait_send()
+
+        @pl.loop(0, S)
+        def _(sec):
+            @pl.loop(1, chips)
+            def _(i):
+                grad_copy(sec, d, other_chip(i)).wait_send()
+
+            @pl.loop(0, chips)
+            def _(i):
+                pair_copy(sec, 2 * i + 1 - core).wait_send()
+
         @pl.loop(1, chips)
         def _(i):
-            grad_copy(sec, d, other_chip(i)).wait_send()
-
-        @pl.loop(0, chips)
+            src = other_chip(i)
+            out_copy(src, d).wait_recv()
+            hand_over(src).start()
+
+        out_copy(partner, d).wait_recv()
+        out_copy(d, partner).wait_send()
+
+        @pl.loop(1, chips)
         def _(i):
-            pair_copy(sec, 2 * i + 1 - core).wait_send()
-
-    @pl.loop(1, chips)
-    def _(i):
-        src = other_chip(i)
-        out_copy(src, d).wait_recv()
-        hand_over(src).start()
-
-    out_copy(partner, d).wait_recv()
-    out_copy(d, partner).wait_send()
-
-    @pl.loop(1, chips)
-    def _(i):
-        out_copy(d, other_chip(i)).wait_send()
-        hand_over(other_chip(i)).wait_send()
-        hand_over(lax.rem(partner + 2 * i, D)).wait_recv()
-
-    new_weights[...] = spread_out[...]
+            out_copy(d, other_chip(i)).wait_send()
+            hand_over(other_chip(i)).wait_send()
+            hand_over(lax.rem(partner + 2 * i, D)).wait_recv()
+
+        new_weights[...] = spread_out[...]
+
+
+def store(a, b, c, out_a, out_b, out_c, sem):
+    copies = [
+        pltpu.make_async_copy(c, out_c, sem.at[2]),
+        pltpu.make_async_copy(a, out_a, sem.at[0]),
+        pltpu.make_async_copy(b, out_b, sem.at[1]),
+    ]
+    for copy in copies:
+        copy.start()
+    for copy in copies:
+        copy.wait()
 
 
 def on_device(S, D, stream, cotangent, weights, master, momentum):
@@ -355,16 +401,16 @@
     rows = master.shape[1]
     bf, f32 = jnp.bfloat16, jnp.float32
     vmem = pl.BlockSpec(memory_space=pltpu.VMEM)
-    hbm = pl.BlockSpec(memory_space=pl.ANY)
+    hbm = pl.BlockSpec(memory_space=pltpu.HBM)
     dma = pltpu.SemaphoreType.DMA
-    new_master, new_momentum, new_weights = pl.pallas_call(
+    results = pl.pallas_call(
         functools.partial(kernel, S, D, per_dp * D),
         out_shape=(
-            jax.ShapeDtypeStruct((rows, C), f32),
-            jax.ShapeDtypeStruct((rows, C), f32),
-            jax.ShapeDtypeStruct((D, rows, C), bf),
+            pltpu.VMEM((rows, C), f32),
+            pltpu.VMEM((rows, C), f32),
+            pltpu.VMEM((D, rows, C), bf),
         ),
-        in_specs=[hbm, hbm, hbm, vmem, vmem],
+        in_specs=[hbm] * 5,
         out_specs=(vmem, vmem, vmem),
         scratch_shapes=[
             pltpu.VMEM((S, R, C), bf),
@@ -381,13 +427,28 @@
             pltpu.VMEM((S, rows, C), bf),
             pltpu.VMEM((rows, C), f32),
             pltpu.VMEM((D, rows, C), bf),
-            dma((4,)), dma, dma((S,)), dma((S,)), dma((S, D)), dma((S, D)), dma((S, D)), dma((S, D)),
+            pltpu.VMEM((rows, C), f32),
+            pltpu.VMEM((rows, C), f32),
+            dma((6,)), dma, dma((S,)), dma((S,)), dma((S, D)), dma((S, D)), dma((S, D)), dma((S, D)),
             dma((S, D)), dma((S, D)), dma((S, D)), dma((S, D)), dma((S,)), dma((S,)),
             dma((D,)), dma((D,)), dma((D,)), dma((D,)),
         ],
         compiler_params=pltpu.CompilerParams(
-            has_side_effects=True, vmem_limit_bytes=61 * 1024 * 1024),
-    )(stream, cotangent, weights[0], master[0], momentum[0])
+            has_side_effects=True, collective_id=0, vmem_limit_bytes=48 * 1024 * 1024),
+    )(*[pltpu.with_memory_space_constraint(x, pltpu.HBM)
+        for x in (stream, cotangent, weights[0], master[0], momentum[0])])
+    new_master, new_momentum, new_weights = pl.pallas_call(
+        store,
+        out_shape=(
+            jax.ShapeDtypeStruct((rows, C), f32),
+            jax.ShapeDtypeStruct((rows, C), f32),
+            jax.ShapeDtypeStruct((D, rows, C), bf),
+        ),
+        in_specs=[vmem] * 3,
+        out_specs=(hbm, hbm, hbm),
+        scratch_shapes=[dma((3,))],
+        compiler_params=pltpu.CompilerParams(vmem_limit_bytes=4 * 1024 * 1024),
+    )(*[pltpu.with_memory_space_constraint(x, pltpu.VMEM) for x in results])
     return (new_master[None], new_momentum[None], new_weights.reshape(1, R, C))
 
 

time: 76.4 us -> 66.6 us (0.87)
  local copies, waits for them, and re-layouts: 5.08 us -> 0 us
  Pallas kernels: 70.5 us -> 65.8 us
    unnamed x3 -> x0, local copies, waits for them, and re-layouts: 5.08 us -> none
    pallas_call x1 -> x2, Pallas kernels: 70.5 us -> 65.8 us  [the longest x1 64.9 us: on_device(): pl.pallas_call(functools.partial(kernel, S, D, per_dp * D), out_shape=(pl...]
where the time goes in v1:
time: 66.6 us; the launch traced here: 66.5 us
  Pallas kernels  65.8 us (99%)
    pallas_call x1, Pallas kernels, on_device(): pl.pallas_call(functools.partial(kernel, S, D, per_dp * D), out_shape=(pl...  64.9 us

profile of v1, /device:TPU:0, one launch (start us, length us, event | category | flops | bytes accessed | tf_op | source)
XLA Modules:
  0.0 66.5 jit_solution(9101170183038515001)
XLA Ops:
  0.6 64.9 %shard_map.76 = (f32[288,128]{1,0:T(8,128)S(1)}, f32[288,128]{1,0:T(8,128)S(1)}, bf16[8,288,128]{2,1,0:T(8,128)(2,1)S(1)}) custom-call(f32[2,8,16,16,128]{4,3,2,1,0:T(8,128)} %stream.1, f32[2,8,16,16,128]{4,3,2,1,0:T(8,128)} %cotangent.1, bf16[2304,128]{1,0:T(8,128)(2,1)} %bitcast.6, f32[288,128]{1,0:T(8,128)} %bitcast.7, f32[288,128]{1,0:T(8,128)} %bitcast.8), custom_call_target="tpu_custom_call" | custom-call | tf_op jit(solution)/shard_map/pallas_call | solution.py:406
  65.5 0.9 %shard_map.77 = (f32[288,128]{1,0:T(8,128)}, f32[288,128]{1,0:T(8,128)}, bf16[8,288,128]{2,1,0:T(8,128)(2,1)}) custom-call(f32[288,128]{1,0:T(8,128)S(1)} %get-tuple-element.9.a, f32[288,128]{1,0:T(8,128)S(1)} %get-tuple-element.10.b, bf16[8,288,128]{2,1,0:T(8,128)(2,1)S(1)} %get-tuple-element.11.c), custom_call_target="tpu_custom_call" | custom-call | tf_op jit(solution)/shard_map/pallas_call | solution.py:440

commit v2 on v0

v2 whole, which is shorter than its diff:
```python
import functools
import math

import jax
import jax.numpy as jnp
from jax import lax
from jax.experimental import pallas as pl
from jax.experimental.pallas import tpu as pltpu
from jax.sharding import PartitionSpec as P

MESH = pl.DeviceIdType.MESH
step_size = 0.1
inertia = 0.9
scope = jax.named_scope


def kernel(
    S, D, images, NP,
    stream, cotangent, weights, master, momentum,
    new_master, new_momentum, new_weights,
    wbuf, xs, ds, pads, kept, slopes, g32, gsend, pairs, recv1, zsend, recv2, gown,
    old_master, old_momentum,
    in_sem, zs, zr, ls, lr, cs, cr, ps, pr, gs, gr, us, ur, os, orr, fs, fr,
):
    s = lax.axis_index("section")
    d = lax.axis_index("dp")
    core = lax.rem(d, 2)
    chip = lax.div(d, 2)
    partner = d + 1 - 2 * core
    chips = D // 2
    HC = chips // 2
    share, H, W, C = xs.shape[1:]
    M = share * H * W
    rows = master.shape[0]
    sub = rows // NP
    R = rows * D
    half = R // 2
    NC = math.gcd(half // 16, D)
    CK = NC // 2
    piece = half // NC
    sends = chip < CK

    def other_chip(i):
        return lax.rem(chip + i, chips)

    def own_piece(h):
        return pl.ds(pl.multiple_of(h * half + (core * CK + chip) * piece, 16), piece)

    def section_copy(sec, h, to):
        return pltpu.make_async_remote_copy(
            src_ref=weights.at[own_piece(h)], dst_ref=wbuf.at[sec, own_piece(h)],
            send_sem=zs, recv_sem=zr.at[sec, h],
            device_id=(to, d), device_id_type=MESH)

    def layer_copy(sec, h, to):
        return pltpu.make_async_remote_copy(
            src_ref=wbuf.at[sec, own_piece(h)], dst_ref=wbuf.at[sec, own_piece(h)],
            send_sem=ls.at[sec, h], recv_sem=lr.at[sec, h],
            device_id=(s, 2 * to + core), device_id_type=MESH)

    def core_copy(sec, h):
        at = pl.ds(pl.multiple_of(h * half + core * (CK * piece), 16), CK * piece)
        return pltpu.make_async_remote_copy(
            src_ref=wbuf.at[sec, at], dst_ref=wbuf.at[sec, at],
            send_sem=cs.at[sec], recv_sem=cr.at[sec, h],
            device_id=(s, partner), device_id_type=MESH)

    def all_of(ref, send_sem, recv_sem):
        return pltpu.make_async_remote_copy(
            src_ref=ref, dst_ref=ref, send_sem=send_sem, recv_sem=recv_sem,
            device_id=(s, partner), device_id_type=MESH)

    def send_down():
        for h in range(2):
            for to in range(S - 1):
                @pl.when(sends & (to < s))
                def _():
                    section_copy(s, h, to).start()

    def send_up():
        for h in range(2):
            for to in range(S - 1, 0, -1):
                @pl.when(sends & (to > s))
                def _():
                    section_copy(s, h, to).start()

    def relay(sec, h):
        @pl.when((sec != s) & (sec < S) & sends)
        def _():
            section_copy(sec, h, s).wait_recv()

            @pl.loop(1, chips)
            def _(i):
                layer_copy(sec, h, other_chip(i)).start()

    def pass_on(sec, h):
        @pl.when((sec != s) & (sec < S))
        def _():
            @pl.when(sends)
            def _():
                all_of(wbuf.at[sec, pl.ds(0, (CK - 1) * piece)], ls.at[sec, h], lr.at[sec, h]).wait_recv()

            if CK < chips:
                @pl.when(chip >= CK)
                def _():
                    all_of(wbuf.at[sec, pl.ds(0, CK * piece)], ls.at[sec, h], lr.at[sec, h]).wait_recv()

            core_copy(sec, h).start()

    def take(sec, h):
        @pl.when(sec != s)
        def _():
            core_copy(sec, h).wait_recv()

    barrier = pltpu.get_barrier_semaphore()

    @pl.loop(1, S)
    def _(i):
        pl.semaphore_signal(barrier, inc=1, device_id=(lax.rem(s + i, S), d), device_id_type=MESH)

    @pl.loop(1, D)
    def _(i):
        pl.semaphore_signal(barrier, inc=1, device_id=(s, lax.rem(d + i, D)), device_id_type=MESH)

    mine = pl.ds(s * share, share)
    loads = [
        pltpu.make_async_copy(stream.at[1, mine], xs.at[1], in_sem.at[1]),
        pltpu.make_async_copy(stream.at[0, mine], xs.at[0], in_sem.at[0]),
        pltpu.make_async_copy(weights, wbuf.at[s], in_sem.at[6]),
        pltpu.make_async_copy(cotangent.at[0, mine], ds.at[0], in_sem.at[2]),
        pltpu.make_async_copy(cotangent.at[1, mine], ds.at[1], in_sem.at[3]),
        pltpu.make_async_copy(momentum, old_momentum, in_sem.at[4]),
        pltpu.make_async_copy(master, old_master, in_sem.at[5]),
    ]
    for load in loads:
        load.start()

    zero_row = jnp.zeros((share, 1, W, 3 * C), jnp.bfloat16)
    for k in range(2):
        pads[k, :, 0:1] = zero_row
        pads[k, :, H + 1 : H + 2] = zero_row

    with scope("t_bar"):
        pl.semaphore_wait(barrier, S + D - 2)
    send_down()

    @pl.when(s == 0)
    def _():
        send_up()

    col = lax.rem(lax.broadcasted_iota(jnp.int32, (M, C), 0), W)

    def shifted(k, flat, order):
        before = jnp.where(col == 0, 0.0, pltpu.roll(flat, 1, 0))
        after = jnp.where(col == W - 1, 0.0, pltpu.roll(flat, M - 1, 0))
        for b, piece_ in enumerate((before, flat, after) if order else (after, flat, before)):
            pads[k, :, 1 : H + 1, :, b * C : (b + 1) * C] = piece_.astype(jnp.bfloat16).reshape(
                share, H, W, C)

    def activate(value, sec, which):
        logistic = 1.0 / (1.0 + jnp.exp(-value))
        act = value * logistic
        slopes[sec, which] = logistic * (1.0 + value * (1.0 - logistic))
        kept[sec, which] = act.astype(jnp.bfloat16)
        shifted(0, act, True)

    def conv(sec, which):
        total = jnp.zeros((M, C), jnp.float32)
        for a in range(3):
            total += jnp.dot(
                pads[0, :, a : a + H].reshape(M, 3 * C),
                wbuf[sec, which * 9 * C + a * 3 * C : which * 9 * C + (a + 1) * 3 * C],
                preferred_element_type=jnp.float32)
        return total

    with scope("t_load"):
        for load in loads[:3]:
            load.wait()
    with scope("t_act"):
        activate(xs[1].reshape(M, C), 0, 0)
    with scope("t_rel"):
        relay(0, 0)

        @pl.when(s > 0)
        def _():
            send_up()

        relay(0, 1)
    with scope("t_pass"):
        pass_on(0, 0)

    def forward_one(sec, carry):
        with scope("t_rel"):
            relay(sec + 1, 0)
        with scope("t_take"):
            take(sec, 0)
        with scope("t_conv"):
            first = xs[0].reshape(M, C) + conv(sec, 0)
        with scope("t_act"):
            activate(first, sec, 1)
            xs[0] = first.reshape(share, H, W, C)
        with scope("t_pass"):
            pass_on(sec, 1)
        with scope("t_rel"):
            relay(sec + 1, 1)
        with scope("t_take"):
            take(sec, 1)
        with scope("t_conv"):
            second = xs[1].reshape(M, C) + conv(sec, 1)

        @pl.when(sec + 1 < S)
        def _():
            with scope("t_act"):
                activate(second, sec + 1, 0)
                xs[1] = second.reshape(share, H, W, C)
            with scope("t_pass"):
                pass_on(sec + 1, 0)

        return carry

    lax.fori_loop(0, S, forward_one, 0)
    for load in loads[3:]:
        load.wait()

    def pair_copy(sec, which):
        at = pl.ds(which * HC, HC)
        return pltpu.make_async_remote_copy(
            src_ref=gsend.at[sec, 1 - core, at], dst_ref=pairs.at[sec, at],
            send_sem=ps.at[sec], recv_sem=pr.at[sec, which],
            device_id=(s, partner), device_id_type=MESH)

    def piece_of(p):
        return pl.ds(p * sub, sub)

    def grad_copy(sec, to, p):
        return pltpu.make_async_remote_copy(
            src_ref=gsend.at[sec, core, to, piece_of(p)], dst_ref=recv1.at[sec, chip, piece_of(p)],
            send_sem=gs.at[sec], recv_sem=gr.at[sec, p],
            device_id=(s, 2 * to + core), device_id_type=MESH)

    def sum_copy(sec, p):
        return pltpu.make_async_remote_copy(
            src_ref=zsend.at[sec, piece_of(p)], dst_ref=recv2.at[s, piece_of(p)],
            send_sem=us, recv_sem=ur.at[p],
            device_id=(sec, d), device_id_type=MESH)

    def wgrad(sec, which):
        rounded = ds[1 if which else 0].reshape(M, C)
        shifted(1, rounded, False)
        act = kept[sec, which]
        for a in range(3):
            block = lax.dot_general(
                act, pads[1, :, 2 - a : 2 - a + H].reshape(M, 3 * C),
                (((0,), (0,)), ((), ())), preferred_element_type=jnp.float32)
            for b in range(3):
                g32[(3 * a + b) * C : (3 * a + b + 1) * C] = block[:, b * C : (b + 1) * C]

        def convert(parity):
            for i in range(HC):
                at = 2 * i + parity
                gsend[sec, parity, which * HC + i] = g32[
                    pl.ds(pl.multiple_of(at * rows, 8), rows)].astype(jnp.bfloat16)

        convert(1 - core)
        pair_copy(sec, which).start()
        convert(core)

    def dgrad(sec, which):
        total = jnp.zeros((M, C), jnp.float32)
        for a in range(3):
            for b in range(3):
                tap = 3 * a + b
                total += lax.dot_general(
                    pads[1, :, 2 - a : 2 - a + H, :, b * C : (b + 1) * C].reshape(M, C),
                    wbuf[sec, which * 9 * C + tap * C : which * 9 * C + (tap + 1) * C],
                    (((1,), (1,)), ((), ())), preferred_element_type=jnp.float32)
        into = 0 if which else 1
        ds[into] = ds[into] + (total * slopes[sec, which]).reshape(share, H, W, C)

    def combine(sec, which):
        pair_copy(sec, which).wait_recv()
        for i in range(HC):
            to = which * HC + i
            both = gsend[sec, core, to].astype(jnp.float32) + pairs[sec, to].astype(jnp.float32)
            gsend[sec, core, to] = both.astype(jnp.bfloat16)

            @pl.when(to != chip)
            def _():
                for p in range(NP):
                    grad_copy(sec, to, p).start()

    def finish(sec, p):
        all_of(recv1.at[sec, pl.ds(0, chips - 1), piece_of(p)], gs.at[sec], gr.at[sec, p]).wait_recv()

        def add(i, total):
            return total + recv1[sec, other_chip(i), piece_of(p)].astype(jnp.float32)

        total = lax.fori_loop(
            1, chips, add, gsend[sec, core, chip, piece_of(p)].astype(jnp.float32))

        @pl.when(sec == s)
        def _():
            gown[piece_of(p)] = total

        @pl.when(sec != s)
        def _():
            zsend[sec, piece_of(p)] = total.astype(jnp.bfloat16)
            sum_copy(sec, p).start()

    def backward_one(turn, carry):
        sec = S - 1 - turn
        with scope("b_wg"):
            wgrad(sec, 1)

        with scope("b_comb"):
            @pl.when(turn > 0)
            def _():
                combine(sec + 1, 0)

        with scope("b_dg"):
            dgrad(sec, 1)
        with scope("b_wg"):
            wgrad(sec, 0)
        with scope("b_comb"):
            combine(sec, 1)

        @pl.when(turn < S - 1)
        def _():
            with scope("b_dg"):
                dgrad(sec, 0)

            @pl.when(turn > 1)
            def _():
                with scope("b_fin"):
                    for p in range(NP):
                        finish(sec + 2, p)

        return carry

    lax.fori_loop(0, S, backward_one, 0)
    with scope("c_comb"):
        combine(0, 0)
    with scope("c_fin1"):
        for sec in range(min(S, 3) - 1, 0, -1):
            for p in range(NP):
                finish(sec, p)
    with scope("c_fin0"):
        for p in range(NP):
            finish(0, p)

    def out_copy(to, p):
        return pltpu.make_async_remote_copy(
            src_ref=new_weights.at[d, piece_of(p)], dst_ref=new_weights.at[d, piece_of(p)],
            send_sem=os, recv_sem=orr.at[p],
            device_id=(s, 2 * to + core), device_id_type=MESH)

    def hand_over(src, p):
        return pltpu.make_async_remote_copy(
            src_ref=new_weights.at[src, piece_of(p)], dst_ref=new_weights.at[src, piece_of(p)],
            send_sem=fs, recv_sem=fr,
            device_id=(s, partner), device_id_type=MESH)

    for p in range(NP):
        with scope("c_sum"):
            all_of(recv2.at[pl.ds(0, S - 1), piece_of(p)], us, ur.at[p]).wait_recv()
        with scope("c_upd"):
            def gather_sums(i, total):
                return total + recv2[lax.rem(s + i, S), piece_of(p)].astype(jnp.float32)

            summed = lax.fori_loop(1, S, gather_sums, gown[piece_of(p)])
            moved = inertia * old_momentum[piece_of(p)] + summed / images
            new_momentum[piece_of(p)] = moved
            fresh = old_master[piece_of(p)] - step_size * moved
            new_master[piece_of(p)] = fresh
            new_weights[d, piece_of(p)] = fresh.astype(jnp.bfloat16)

            @pl.loop(1, chips)
            def _(i):
                out_copy(other_chip(i), p).start()

            hand_over(d, p).start()

    with scope("c_sent"):
        @pl.when(sends)
        def _():
            all_of(wbuf.at[0, pl.ds(0, 2 * (S - 1) * piece)], zs, zr.at[0, 0]).wait_send()

        @pl.loop(0, S)
        def _(sec):
            @pl.when(sec != s)
            def _():
                @pl.when(sends)
                def _():
                    for h in range(2):
                        all_of(wbuf.at[sec, pl.ds(0, (chips - 1) * piece)], ls.at[sec, h], lr.at[sec, h]).wait_send()

                all_of(wbuf.at[sec, pl.ds(0, 2 * CK * piece)], cs.at[sec], cr.at[sec, 0]).wait_send()

            all_of(gsend.at[sec, 0], ps.at[sec], pr.at[sec, 0]).wait_send()
            all_of(recv1.at[sec, pl.ds(0, chips - 1)], gs.at[sec], gr.at[sec, 0]).wait_send()

        all_of(recv2.at[pl.ds(0, S - 1)], us, ur.at[0]).wait_send()

    for p in range(NP):
        with scope("c_orecv"):
            all_of(recv1.at[0, pl.ds(0, chips - 1), piece_of(p)], os, orr.at[p]).wait_recv()

        @pl.loop(1, chips)
        def _(i):
            hand_over(2 * other_chip(i) + core, p).start()

    with scope("c_end"):
        all_of(recv1.at[0, pl.ds(0, chips - 1)], os, orr.at[0]).wait_send()
        all_of(recv1.at[0], fs, fr).wait_send()
        all_of(recv1.at[0], fs, fr).wait_recv()


def store(a, b, c, out_a, out_b, out_c, sem):
    copies = [
        pltpu.make_async_copy(c, out_c, sem.at[2]),
        pltpu.make_async_copy(a, out_a, sem.at[0]),
        pltpu.make_async_copy(b, out_b, sem.at[1]),
    ]
    for copy in copies:
        copy.start()
    for copy in copies:
        copy.wait()


def on_device(S, D, stream, cotangent, weights, master, momentum):
    _, per_dp, H, W, C = stream.shape
    share = per_dp // S
    M = share * H * W
    R = weights.shape[1]
    rows = master.shape[1]
    chips = D // 2
    NP = 3 if rows % 48 == 0 else 1
    bf, f32 = jnp.bfloat16, jnp.float32
    vmem = pl.BlockSpec(memory_space=pltpu.VMEM)
    hbm = pl.BlockSpec(memory_space=pltpu.HBM)
    dma = pltpu.SemaphoreType.DMA
    results = pl.pallas_call(
        functools.partial(kernel, S, D, per_dp * D, NP),
        out_shape=(
            pltpu.VMEM((rows, C), f32),
            pltpu.VMEM((rows, C), f32),
            pltpu.VMEM((D, rows, C), bf),
        ),
        in_specs=[hbm] * 5,
        out_specs=(vmem, vmem, vmem),
        scratch_shapes=[
            pltpu.VMEM((S, R, C), bf),
            pltpu.VMEM((2, share, H, W, C), f32),
            pltpu.VMEM((2, share, H, W, C), f32),
            pltpu.VMEM((2, share, H + 2, W, 3 * C), bf),
            pltpu.VMEM((S, 2, M, C), bf),
            pltpu.VMEM((S, 2, M, C), f32),
            pltpu.VMEM((R // 2, C), f32),
            pltpu.VMEM((S, 2, chips, rows, C), bf),
            pltpu.VMEM((S, chips, rows, C), bf),
            pltpu.VMEM((S, chips, rows, C), bf),
            pltpu.VMEM((S, rows, C), bf),
            pltpu.VMEM((S, rows, C), bf),
            pltpu.VMEM((rows, C), f32),
            pltpu.VMEM((rows, C), f32),
            pltpu.VMEM((rows, C), f32),
            dma((7,)), dma, dma((S, 2)), dma((S, 2)), dma((S, 2)), dma((S,)), dma((S, 2)),
            dma((S,)), dma((S, 2)), dma((S,)), dma((S, NP)), dma, dma((NP,)),
            dma, dma((NP,)), dma, dma,
        ],
        compiler_params=pltpu.CompilerParams(
            has_side_effects=True, collective_id=0, vmem_limit_bytes=48 * 1024 * 1024),
    )(*[pltpu.with_memory_space_constraint(x, pltpu.HBM)
        for x in (stream, cotangent, weights[0], master[0], momentum[0])])
    new_master, new_momentum, new_weights = pl.pallas_call(
        store,
        out_shape=(
            jax.ShapeDtypeStruct((rows, C), f32),
            jax.ShapeDtypeStruct((rows, C), f32),
            jax.ShapeDtypeStruct((D, rows, C), bf),
        ),
        in_specs=[vmem] * 3,
        out_specs=(hbm, hbm, hbm),
        scratch_shapes=[dma((3,))],
        compiler_params=pltpu.CompilerParams(vmem_limit_bytes=4 * 1024 * 1024),
    )(*[pltpu.with_memory_space_constraint(x, pltpu.VMEM) for x in results])
    return (new_master[None], new_momentum[None], new_weights.reshape(1, R, C))


def solution(mesh):
    placed = (
        P(None, "dp", None, None, None),
        P(None, "dp", None, None, None),
        P("section", None, None),
        P("section", "dp", None),
        P("section", "dp", None),
    )
    return jax.shard_map(
        functools.partial(on_device, mesh.shape["section"], mesh.shape["dp"]),
        mesh=mesh,
        in_specs=placed,
        out_specs=(P("section", "dp", None), P("section", "dp", None), P("section", None, None)),
        check_vma=False,
    )
```

time: 76.4 us -> 58.9 us (0.77)
  Pallas kernels: 70.5 us -> 58.1 us
  local copies, waits for them, and re-layouts: 5.08 us -> 0 us
    pallas_call x1 -> x2, Pallas kernels: 70.5 us -> 58.1 us  [the longest x1 57.1 us: on_device(): pl.pallas_call(functools.partial(kernel, S, D, per_dp * D, NP), out_shape...]
    unnamed x3 -> x0, local copies, waits for them, and re-layouts: 5.08 us -> none
where the time goes in v2:
time: 58.9 us; the launch traced here: 58.7 us
  Pallas kernels  58.1 us (99%)
  between operations  0.64 us (1%)
    pallas_call x1, Pallas kernels, on_device(): pl.pallas_call(functools.partial(kernel, S, D, per_dp * D, NP), out_shape...  57.1 us

profile of v2, /device:TPU:0, one launch (start us, length us, event | category | flops | bytes accessed | tf_op | source)
XLA Modules:
  0.0 58.7 jit_solution(14369794960266611475)
XLA Ops:
  0.6 57.1 %shard_map.76 = (f32[288,128]{1,0:T(8,128)S(1)}, f32[288,128]{1,0:T(8,128)S(1)}, bf16[8,288,128]{2,1,0:T(8,128)(2,1)S(1)}) custom-call(f32[2,8,16,16,128]{4,3,2,1,0:T(8,128)} %stream.1, f32[2,8,16,16,128]{4,3,2,1,0:T(8,128)} %cotangent.1, bf16[2304,128]{1,0:T(8,128)(2,1)} %bitcast.6, f32[288,128]{1,0:T(8,128)} %bitcast.7, f32[288,128]{1,0:T(8,128)} %bitcast.8), custom_call_target="tpu_custom_call" | custom-call | tf_op jit(solution)/shard_map/pallas_call | solution.py:442
  57.8 0.9 %shard_map.77 = (f32[288,128]{1,0:T(8,128)}, f32[288,128]{1,0:T(8,128)}, bf16[8,288,128]{2,1,0:T(8,128)(2,1)}) custom-call(f32[288,128]{1,0:T(8,128)S(1)} %get-tuple-element.9.a, f32[288,128]{1,0:T(8,128)S(1)} %get-tuple-element.10.b, bf16[8,288,128]{2,1,0:T(8,128)(2,1)S(1)} %get-tuple-element.11.c), custom_call_target="tpu_custom_call" | custom-call | tf_op jit(solution)/shard_map/pallas_call | solution.py:475

commit v3 on v2

--- a/solution.py
+++ b/solution.py
@@ -18,9 +18,9 @@
     S, D, images, NP,
     stream, cotangent, weights, master, momentum,
     new_master, new_momentum, new_weights,
-    wbuf, xs, ds, pads, kept, slopes, g32, gsend, pairs, recv1, zsend, recv2, gown,
+    wbuf, xs, ds, patches, turned, slopes, g32, gsend, pairs, recv1, zsend, recv2, recv3, gown,
     old_master, old_momentum,
-    in_sem, zs, zr, ls, lr, cs, cr, ps, pr, gs, gr, us, ur, os, orr, fs, fr,
+    in_sem, zs, zr, ls, lr, cs, cr, ps, pr, gs, gr, us, ur, vr, os, orr, fs, fr,
 ):
     s = lax.axis_index("section")
     d = lax.axis_index("dp")
@@ -39,6 +39,11 @@
     CK = NC // 2
     piece = half // NC
     sends = chip < CK
+    square = chips == 4
+    across = chip + 1 - 2 * lax.rem(chip, 2)
+    along = lax.rem(chip + HC, chips)
+    near = across + core * (along - across)
+    far = along + core * (across - along)
 
     def other_chip(i):
         return lax.rem(chip + i, chips)
@@ -77,12 +82,16 @@
                 def _():
                     section_copy(s, h, to).start()
 
-    def send_up():
-        for h in range(2):
-            for to in range(S - 1, 0, -1):
-                @pl.when(sends & (to > s))
-                def _():
-                    section_copy(s, h, to).start()
+    def send_top(h):
+        @pl.when(sends & (s < S - 1))
+        def _():
+            section_copy(s, h, S - 1).start()
+
+    def send_up(h):
+        for to in range(S - 2, 0, -1):
+            @pl.when(sends & (to > s))
+            def _():
+                section_copy(s, h, to).start()
 
     def relay(sec, h):
         @pl.when((sec != s) & (sec < S) & sends)
@@ -135,43 +144,46 @@
     for load in loads:
         load.start()
 
-    zero_row = jnp.zeros((share, 1, W, 3 * C), jnp.bfloat16)
-    for k in range(2):
-        pads[k, :, 0:1] = zero_row
-        pads[k, :, H + 1 : H + 2] = zero_row
-
     with scope("t_bar"):
         pl.semaphore_wait(barrier, S + D - 2)
+    send_top(0)
     send_down()
 
     @pl.when(s == 0)
     def _():
-        send_up()
+        send_up(0)
+        send_top(1)
+        send_up(1)
 
     col = lax.rem(lax.broadcasted_iota(jnp.int32, (M, C), 0), W)
 
-    def shifted(k, flat, order):
+    def column_taps(flat):
         before = jnp.where(col == 0, 0.0, pltpu.roll(flat, 1, 0))
         after = jnp.where(col == W - 1, 0.0, pltpu.roll(flat, M - 1, 0))
-        for b, piece_ in enumerate((before, flat, after) if order else (after, flat, before)):
-            pads[k, :, 1 : H + 1, :, b * C : (b + 1) * C] = piece_.astype(jnp.bfloat16).reshape(
-                share, H, W, C)
+        return [x.astype(jnp.bfloat16) for x in (before, flat, after)]
+
+    def row_moved(flat, by):
+        if by == 0:
+            return flat
+        field = flat.reshape(share, H, W, C)
+        edge = jnp.zeros((share, 1, W, C), flat.dtype)
+        parts = (edge, field[:, : H - 1]) if by > 0 else (field[:, 1:], edge)
+        return jnp.concatenate(parts, axis=1).reshape(M, C)
 
     def activate(value, sec, which):
         logistic = 1.0 / (1.0 + jnp.exp(-value))
         act = value * logistic
         slopes[sec, which] = logistic * (1.0 + value * (1.0 - logistic))
-        kept[sec, which] = act.astype(jnp.bfloat16)
-        shifted(0, act, True)
+        for b, tap in enumerate(column_taps(act)):
+            patches[:, b * C : (b + 1) * C] = tap
+            turned[sec, which, b * C : (b + 1) * C] = tap.T
 
     def conv(sec, which):
-        total = jnp.zeros((M, C), jnp.float32)
-        for a in range(3):
-            total += jnp.dot(
-                pads[0, :, a : a + H].reshape(M, 3 * C),
-                wbuf[sec, which * 9 * C + a * 3 * C : which * 9 * C + (a + 1) * 3 * C],
-                preferred_element_type=jnp.float32)
-        return total
+        wide = jnp.concatenate(
+            [wbuf[sec, which * 9 * C + a * 3 * C : which * 9 * C + (a + 1) * 3 * C] for a in range(3)],
+            axis=1)
+        found = jnp.dot(patches[...], wide, preferred_element_type=jnp.float32)
+        return sum(row_moved(found[:, a * C : (a + 1) * C], 1 - a) for a in range(3))
 
     with scope("t_load"):
         for load in loads[:3]:
@@ -183,28 +195,43 @@
 
         @pl.when(s > 0)
         def _():
-            send_up()
+            send_top(1)
+            send_up(0)
+            send_up(1)
 
         relay(0, 1)
+        relay(1, 0)
     with scope("t_pass"):
         pass_on(0, 0)
 
     def forward_one(sec, carry):
         with scope("t_rel"):
-            relay(sec + 1, 0)
+            relay(sec + 1, 1)
         with scope("t_take"):
             take(sec, 0)
+
+        @pl.when(sec > 0)
+        def _():
+            with scope("t_pass"):
+                pass_on(sec, 1)
+
         with scope("t_conv"):
             first = xs[0].reshape(M, C) + conv(sec, 0)
         with scope("t_act"):
             activate(first, sec, 1)
             xs[0] = first.reshape(share, H, W, C)
-        with scope("t_pass"):
-            pass_on(sec, 1)
+
+        @pl.when(sec == 0)
+        def _():
+            with scope("t_pass"):
+                pass_on(sec, 1)
+
         with scope("t_rel"):
-            relay(sec + 1, 1)
+            relay(sec + 2, 0)
         with scope("t_take"):
             take(sec, 1)
+        with scope("t_pass"):
+            pass_on(sec + 1, 0)
         with scope("t_conv"):
             second = xs[1].reshape(M, C) + conv(sec, 1)
 
@@ -213,8 +240,6 @@
             with scope("t_act"):
                 activate(second, sec + 1, 0)
                 xs[1] = second.reshape(share, H, W, C)
-            with scope("t_pass"):
-                pass_on(sec + 1, 0)
 
         return carry
 
@@ -238,22 +263,38 @@
             send_sem=gs.at[sec], recv_sem=gr.at[sec, p],
             device_id=(s, 2 * to + core), device_id_type=MESH)
 
+    def near_copy(sec, piece_, slot):
+        return pltpu.make_async_remote_copy(
+            src_ref=gsend.at[sec, core, piece_], dst_ref=recv1.at[sec, slot],
+            send_sem=gs.at[sec], recv_sem=gr.at[sec, 0],
+            device_id=(s, 2 * near + core), device_id_type=MESH)
+
+    def far_copy(sec):
+        return pltpu.make_async_remote_copy(
+            src_ref=gsend.at[sec, core, far], dst_ref=recv1.at[sec, 2],
+            send_sem=gs.at[sec], recv_sem=gr.at[sec, 1],
+            device_id=(s, 2 * far + core), device_id_type=MESH)
+
     def sum_copy(sec, p):
         return pltpu.make_async_remote_copy(
             src_ref=zsend.at[sec, piece_of(p)], dst_ref=recv2.at[s, piece_of(p)],
             send_sem=us, recv_sem=ur.at[p],
             device_id=(sec, d), device_id_type=MESH)
 
+    def step_copy(p):
+        return pltpu.make_async_remote_copy(
+            src_ref=zsend.at[0, piece_of(p)], dst_ref=recv3.at[piece_of(p)],
+            send_sem=us, recv_sem=vr.at[p],
+            device_id=(s - 1, d), device_id_type=MESH)
+
     def wgrad(sec, which):
-        rounded = ds[1 if which else 0].reshape(M, C)
-        shifted(1, rounded, False)
-        act = kept[sec, which]
+        rounded = ds[1 if which else 0].reshape(M, C).astype(jnp.bfloat16)
+        moved = jnp.concatenate([row_moved(rounded, a - 1) for a in range(3)], axis=1)
+        found = jnp.dot(turned[sec, which], moved, preferred_element_type=jnp.float32)
         for a in range(3):
-            block = lax.dot_general(
-                act, pads[1, :, 2 - a : 2 - a + H].reshape(M, 3 * C),
-                (((0,), (0,)), ((), ())), preferred_element_type=jnp.float32)
             for b in range(3):
-                g32[(3 * a + b) * C : (3 * a + b + 1) * C] = block[:, b * C : (b + 1) * C]
+                g32[(3 * a + b) * C : (3 * a + b + 1) * C] = found[
+                    b * C : (b + 1) * C, a * C : (a + 1) * C]
 
         def convert(parity):
             for i in range(HC):
@@ -266,46 +307,99 @@
         convert(core)
 
     def dgrad(sec, which):
-        total = jnp.zeros((M, C), jnp.float32)
-        for a in range(3):
-            for b in range(3):
-                tap = 3 * a + b
-                total += lax.dot_general(
-                    pads[1, :, 2 - a : 2 - a + H, :, b * C : (b + 1) * C].reshape(M, C),
-                    wbuf[sec, which * 9 * C + tap * C : which * 9 * C + (tap + 1) * C],
-                    (((1,), (1,)), ((), ())), preferred_element_type=jnp.float32)
+        before, at, after = column_taps(ds[1 if which else 0].reshape(M, C))
+        wide = jnp.concatenate([after, at, before], axis=1)
+        taps = wbuf[sec, which * 9 * C : (which + 1) * 9 * C].reshape(3, 3, C, C)
+        turn = jnp.concatenate(
+            [jnp.concatenate([taps[a, b] for b in range(3)], axis=1) for a in range(3)], axis=0)
+        found = lax.dot_general(
+            wide, turn, (((1,), (1,)), ((), ())), preferred_element_type=jnp.float32)
+        total = sum(row_moved(found[:, a * C : (a + 1) * C], a - 1) for a in range(3))
         into = 0 if which else 1
         ds[into] = ds[into] + (total * slopes[sec, which]).reshape(share, H, W, C)
 
     def combine(sec, which):
+        direct = sec == 0 if square else True
         pair_copy(sec, which).wait_recv()
         for i in range(HC):
             to = which * HC + i
             both = gsend[sec, core, to].astype(jnp.float32) + pairs[sec, to].astype(jnp.float32)
             gsend[sec, core, to] = both.astype(jnp.bfloat16)
 
-            @pl.when(to != chip)
+            @pl.when((to != chip) & direct)
             def _():
                 for p in range(NP):
                     grad_copy(sec, to, p).start()
 
-    def finish(sec, p):
+            if square:
+                @pl.when((to == near) & (sec != 0))
+                def _():
+                    near_copy(sec, to, 0).start()
+
+                @pl.when((to == chips - 1 - chip) & (sec != 0))
+                def _():
+                    near_copy(sec, to, 1).start()
+
+    def step(sec):
+        if square:
+            all_of(recv1.at[sec, pl.ds(0, 2)], gs.at[sec], gr.at[sec, 0]).wait_recv()
+            both = gsend[sec, core, far].astype(jnp.float32) + recv1[sec, 1].astype(jnp.float32)
+            gsend[sec, core, far] = both.astype(jnp.bfloat16)
+            far_copy(sec).start()
+
+    def hand_in(sec, p, total):
+        @pl.when(sec == s)
+        def _():
+            gown[piece_of(p)] = total
+
+        @pl.when(sec != s)
+        def _():
+            zsend[sec, piece_of(p)] = total.astype(jnp.bfloat16)
+            sum_copy(sec, p).start()
+
+    def plane_sum(sec, p):
         all_of(recv1.at[sec, pl.ds(0, chips - 1), piece_of(p)], gs.at[sec], gr.at[sec, p]).wait_recv()
 
         def add(i, total):
             return total + recv1[sec, other_chip(i), piece_of(p)].astype(jnp.float32)
 
-        total = lax.fori_loop(
+        return lax.fori_loop(
             1, chips, add, gsend[sec, core, chip, piece_of(p)].astype(jnp.float32))
 
-        @pl.when(sec == s)
+    def finish(sec):
+        if square:
+            all_of(recv1.at[sec, 2], gs.at[sec], gr.at[sec, 1]).wait_recv()
+        for p in range(NP):
+            if square:
+                total = sum(
+                    ref[piece_of(p)].astype(jnp.float32)
+                    for ref in (gsend.at[sec, core, chip], recv1.at[sec, 0], recv1.at[sec, 2]))
+            else:
+                total = plane_sum(sec, p)
+            hand_in(sec, p, total)
+
+    def finish_last(p):
+        total = plane_sum(0, p)
+
+        @pl.when(s == 0)
         def _():
             gown[piece_of(p)] = total
 
-        @pl.when(sec != s)
-        def _():
-            zsend[sec, piece_of(p)] = total.astype(jnp.bfloat16)
-            sum_copy(sec, p).start()
+        @pl.when((s > 1) & (lax.rem(s, 2) == 1))
+        def _():
+            zsend[0, piece_of(p)] = total.astype(jnp.bfloat16)
+            step_copy(p).start()
+
+        @pl.when((s == 1) | ((s == S - 1) & (lax.rem(s, 2) == 0)))
+        def _():
+            zsend[0, piece_of(p)] = total.astype(jnp.bfloat16)
+            sum_copy(0, p).start()
+
+        @pl.when((s > 0) & (s < S - 1) & (lax.rem(s, 2) == 0))
+        def _():
+            step_copy(p).wait_recv()
+            zsend[0, piece_of(p)] = (total + recv3[piece_of(p)].astype(jnp.float32)).astype(jnp.bfloat16)
+            sum_copy(0, p).start()
 
     def backward_one(turn, carry):
         sec = S - 1 - turn
@@ -329,24 +423,33 @@
             with scope("b_dg"):
                 dgrad(sec, 0)
 
-            @pl.when(turn > 1)
-            def _():
-                with scope("b_fin"):
-                    for p in range(NP):
-                        finish(sec + 2, p)
+        @pl.when(turn > 1)
+        def _():
+            with scope("b_step"):
+                step(sec + 2)
+
+        @pl.when(turn > 3)
+        def _():
+            with scope("b_fin"):
+                finish(sec + 4)
 
         return carry
 
     lax.fori_loop(0, S, backward_one, 0)
     with scope("c_comb"):
         combine(0, 0)
+    with scope("c_step"):
+        if S > 1:
+            step(1)
     with scope("c_fin1"):
-        for sec in range(min(S, 3) - 1, 0, -1):
-            for p in range(NP):
-                finish(sec, p)
+        for sec in range(min(S, 4) - 1, 1, -1):
+            finish(sec)
     with scope("c_fin0"):
         for p in range(NP):
-            finish(0, p)
+            finish_last(p)
+    with scope("c_fin2"):
+        if S > 1:
+            finish(1)
 
     def out_copy(to, p):
         return pltpu.make_async_remote_copy(
@@ -360,14 +463,26 @@
             send_sem=fs, recv_sem=fr,
             device_id=(s, partner), device_id_type=MESH)
 
+    few = 1 + (S - 1) // 2
+    parts = jnp.where(s == 0, few, S - 1)
+
+    def part(i):
+        return jnp.where(s == 0, jnp.maximum(2 * i, 1), lax.rem(s + i + 1, S))
+
     for p in range(NP):
         with scope("c_sum"):
-            all_of(recv2.at[pl.ds(0, S - 1), piece_of(p)], us, ur.at[p]).wait_recv()
+            @pl.when(s == 0)
+            def _():
+                all_of(recv2.at[pl.ds(0, few), piece_of(p)], us, ur.at[p]).wait_recv()
+
+            @pl.when(s != 0)
+            def _():
+                all_of(recv2.at[pl.ds(0, S - 1), piece_of(p)], us, ur.at[p]).wait_recv()
         with scope("c_upd"):
             def gather_sums(i, total):
-                return total + recv2[lax.rem(s + i, S), piece_of(p)].astype(jnp.float32)
-
-            summed = lax.fori_loop(1, S, gather_sums, gown[piece_of(p)])
+                return total + recv2[part(i), piece_of(p)].astype(jnp.float32)
+
+            summed = lax.fori_loop(0, parts, gather_sums, gown[piece_of(p)])
             moved = inertia * old_momentum[piece_of(p)] + summed / images
             new_momentum[piece_of(p)] = moved
             fresh = old_master[piece_of(p)] - step_size * moved
@@ -452,8 +567,8 @@
             pltpu.VMEM((S, R, C), bf),
             pltpu.VMEM((2, share, H, W, C), f32),
             pltpu.VMEM((2, share, H, W, C), f32),
-            pltpu.VMEM((2, share, H + 2, W, 3 * C), bf),
-            pltpu.VMEM((S, 2, M, C), bf),
+            pltpu.VMEM((M, 3 * C), bf),
+            pltpu.VMEM((S, 2, 3 * C, M), bf),
             pltpu.VMEM((S, 2, M, C), f32),
             pltpu.VMEM((R // 2, C), f32),
             pltpu.VMEM((S, 2, chips, rows, C), bf),
@@ -461,11 +576,12 @@
             pltpu.VMEM((S, chips, rows, C), bf),
             pltpu.VMEM((S, rows, C), bf),
             pltpu.VMEM((S, rows, C), bf),
+            pltpu.VMEM((rows, C), bf),
             pltpu.VMEM((rows, C), f32),
             pltpu.VMEM((rows, C), f32),
             pltpu.VMEM((rows, C), f32),
             dma((7,)), dma, dma((S, 2)), dma((S, 2)), dma((S, 2)), dma((S,)), dma((S, 2)),
-            dma((S,)), dma((S, 2)), dma((S,)), dma((S, NP)), dma, dma((NP,)),
+            dma((S,)), dma((S, 2)), dma((S,)), dma((S, max(NP, 2))), dma, dma((NP,)), dma((NP,)),
             dma, dma((NP,)), dma, dma,
         ],
         compiler_params=pltpu.CompilerParams(

time: 58.9 us -> 54.6 us (0.927)
  Pallas kernels: 58.1 us -> 53.8 us
    pallas_call x1, Pallas kernels: 57.1 us -> 52.9 us  [on_device(): pl.pallas_call(functools.partial(kernel, S, D, per_dp * D, NP), out_shape...]
where the time goes in v3:
time: 54.6 us; the launch traced here: 54.4 us
  Pallas kernels  53.8 us (99%)
  between operations  0.64 us (1%)
    pallas_call x1, Pallas kernels, on_device(): pl.pallas_call(functools.partial(kernel, S, D, per_dp * D, NP), out_shape...  52.9 us

profile of v3, /device:TPU:0, one launch (start us, length us, event | category | flops | bytes accessed | tf_op | source)
XLA Modules:
  0.0 54.4 jit_solution(735349235062546864)
XLA Ops:
  0.6 52.9 %shard_map.76 = (f32[288,128]{1,0:T(8,128)S(1)}, f32[288,128]{1,0:T(8,128)S(1)}, bf16[8,288,128]{2,1,0:T(8,128)(2,1)S(1)}) custom-call(f32[2,8,16,16,128]{4,3,2,1,0:T(8,128)} %stream.1, f32[2,8,16,16,128]{4,3,2,1,0:T(8,128)} %cotangent.1, bf16[2304,128]{1,0:T(8,128)(2,1)} %bitcast.6, f32[288,128]{1,0:T(8,128)} %bitcast.7, f32[288,128]{1,0:T(8,128)} %bitcast.8), custom_call_target="tpu_custom_call" | custom-call | tf_op jit(solution)/shard_map/pallas_call | solution.py:557
  53.5 0.9 %shard_map.77 = (f32[288,128]{1,0:T(8,128)}, f32[288,128]{1,0:T(8,128)}, bf16[8,288,128]{2,1,0:T(8,128)(2,1)}) custom-call(f32[288,128]{1,0:T(8,128)S(1)} %get-tuple-element.9.a, f32[288,128]{1,0:T(8,128)S(1)} %get-tuple-element.10.b, bf16[8,288,128]{2,1,0:T(8,128)(2,1)S(1)} %get-tuple-element.11.c), custom_call_target="tpu_custom_call" | custom-call | tf_op jit(solution)/shard_map/pallas_call | solution.py:591
